TPU v7x, 32 devices: a whole 2x2x4 slice. The times are simulated.
32 devices in a mesh: batch: 8 (over y, x, core), cols: 4 (over z).
Axes of the slice: x: 2, y: 2, z: 4, core: 2. Of those that a mesh axis runs over, the one named last changes fastest.
Arguments:
- grad_up: float32 [8, 1024, 4096], P('batch', None, 'cols'), may hold values from -0.875 to 0.875
- grad_down: float32 [8, 4096, 1024], P('batch', 'cols'), may hold values from -0.875 to 0.875
- grad_query: float32 [8, 1024, 1024], P('batch', None, 'cols'), may hold values from -0.875 to 0.875
- grad_key: float32 [8, 1024, 1024], P('batch', None, 'cols'), may hold values from -0.875 to 0.875
- grad_value: float32 [8, 1024, 1024], P('batch', None, 'cols'), may hold values from -0.875 to 0.875
- grad_mixed: float32 [8, 1024, 1024], P('batch', 'cols'), may hold values from -0.875 to 0.875
- grad_norm: float32 [8, 1024], P('batch'), may hold values from -8 to 8
- weight_up: float32 [1024, 4096], P('batch', 'cols'), may hold values from -0.1875 to 0.1875
- weight_down: float32 [4096, 1024], P('cols', 'batch'), may hold values from -0.09375 to 0.09375
- weight_query: float32 [1024, 1024], P('batch', 'cols'), may hold values from -0.1875 to 0.1875
- weight_key: float32 [1024, 1024], P('batch', 'cols'), may hold values from -0.1875 to 0.1875
- weight_value: float32 [1024, 1024], P('batch', 'cols'), may hold values from -0.1875 to 0.1875
- weight_mixed: float32 [1024, 1024], P('cols', 'batch'), may hold values from -0.1875 to 0.1875
- weight_norm: float32 [1024], P('batch'), may hold values from 0.25 to 1.75
- moment_up: float32 [1024, 4096], P('batch', 'cols'), may hold values from -1.75 to 1.75
- moment_down: float32 [4096, 1024], P('cols', 'batch'), may hold values from -1.75 to 1.75
- moment_query: float32 [1024, 1024], P('batch', 'cols'), may hold values from -1.75 to 1.75
- moment_key: float32 [1024, 1024], P('batch', 'cols'), may hold values from -1.75 to 1.75
- moment_value: float32 [1024, 1024], P('batch', 'cols'), may hold values from -1.75 to 1.75
- moment_mixed: float32 [1024, 1024], P('cols', 'batch'), may hold values from -1.75 to 1.75
- moment_norm: float32 [1024], P('batch'), may hold values from -1.75 to 1.75
Outputs:
- copy_up: bfloat16 [1024, 4096], P(None, 'cols')
- copy_down: bfloat16 [4096, 1024], P('cols')
- copy_query: bfloat16 [1024, 1024], P(None, 'cols')
- copy_key: bfloat16 [1024, 1024], P(None, 'cols')
- copy_value: bfloat16 [1024, 1024], P(None, 'cols')
- copy_mixed: bfloat16 [1024, 1024], P('cols')
- copy_norm: bfloat16 [1024], replicated
- new_up: float32 [1024, 4096], P('batch', 'cols')
- new_down: float32 [4096, 1024], P('cols', 'batch')
- new_query: float32 [1024, 1024], P('batch', 'cols')
- new_key: float32 [1024, 1024], P('batch', 'cols')
- new_value: float32 [1024, 1024], P('batch', 'cols')
- new_mixed: float32 [1024, 1024], P('cols', 'batch')
- new_norm: float32 [1024], P('batch')
- state_new_up: float32 [1024, 4096], P('batch', 'cols')
- state_new_down: float32 [4096, 1024], P('cols', 'batch')
- state_new_query: float32 [1024, 1024], P('batch', 'cols')
- state_new_key: float32 [1024, 1024], P('batch', 'cols')
- state_new_value: float32 [1024, 1024], P('batch', 'cols')
- state_new_mixed: float32 [1024, 1024], P('cols', 'batch')
- state_new_norm: float32 [1024], P('batch')
All inputs are finite; a program needn't handle non-finite values.
Results may differ from a plain program's by a relative error of at most 0.008.
Values may be sent and summed in bfloat16 or wider, within the bound.
A program may use at most 64 MiB of HBM per device.

v0:
```python
import jax
import jax.numpy as jnp
from jax import lax
from jax.sharding import PartitionSpec as P

learn_rate = 0.1
hold_rate = 0.7


def body(
    grad_up,
    grad_down,
    grad_query,
    grad_key,
    grad_value,
    grad_mixed,
    grad_norm,
    weight_up,
    weight_down,
    weight_query,
    weight_key,
    weight_value,
    weight_mixed,
    weight_norm,
    moment_up,
    moment_down,
    moment_query,
    moment_key,
    moment_value,
    moment_mixed,
    moment_norm,
):
    mean_up, mean_down, mean_query, mean_key, mean_value, mean_mixed = (
        lax.psum_scatter(
            grad_up[0].astype(jnp.bfloat16), "batch", scatter_dimension=0, tiled=True
        ).astype(jnp.float32),
        lax.psum_scatter(
            grad_down[0].astype(jnp.bfloat16), "batch", scatter_dimension=1, tiled=True
        ).astype(jnp.float32),
        lax.psum_scatter(
            grad_query[0].astype(jnp.bfloat16), "batch", scatter_dimension=0, tiled=True
        ).astype(jnp.float32),
        lax.psum_scatter(
            grad_key[0].astype(jnp.bfloat16), "batch", scatter_dimension=0, tiled=True
        ).astype(jnp.float32),
        lax.psum_scatter(
            grad_value[0].astype(jnp.bfloat16), "batch", scatter_dimension=0, tiled=True
        ).astype(jnp.float32),
        lax.psum_scatter(
            grad_mixed[0].astype(jnp.bfloat16), "batch", scatter_dimension=1, tiled=True
        ).astype(jnp.float32),
    )
    whole_norm = lax.psum(grad_norm[0], "batch")
    place = lax.axis_index("batch")
    mean_norm = lax.dynamic_slice_in_dim(
        whole_norm, place * weight_norm.shape[0], weight_norm.shape[0]
    )
    mean_rate = lax.axis_size("batch") ** (-0.5)
    mean_up = mean_up * mean_rate
    mean_down = mean_down * mean_rate
    mean_query = mean_query * mean_rate
    mean_key = mean_key * mean_rate
    mean_value = mean_value * mean_rate
    mean_mixed = mean_mixed * mean_rate
    mean_norm = mean_norm * mean_rate
    state_new_up = hold_rate * moment_up + mean_up
    new_up = weight_up - learn_rate * state_new_up
    state_new_down = hold_rate * moment_down + mean_down
    new_down = weight_down - learn_rate * state_new_down
    state_new_query = hold_rate * moment_query + mean_query
    new_query = weight_query - learn_rate * state_new_query
    state_new_key = hold_rate * moment_key + mean_key
    new_key = weight_key - learn_rate * state_new_key
    state_new_value = hold_rate * moment_value + mean_value
    new_value = weight_value - learn_rate * state_new_value
    state_new_mixed = hold_rate * moment_mixed + mean_mixed
    new_mixed = weight_mixed - learn_rate * state_new_mixed
    state_new_norm = hold_rate * moment_norm + mean_norm
    new_norm = weight_norm - learn_rate * state_new_norm
    copy_up, copy_down, copy_query, copy_key, copy_value, copy_mixed, copy_norm = (
        lax.all_gather(new_up.astype(jnp.bfloat16), "batch", axis=0, tiled=True),
        lax.all_gather(new_down.astype(jnp.bfloat16), "batch", axis=1, tiled=True),
        lax.all_gather(new_query.astype(jnp.bfloat16), "batch", axis=0, tiled=True),
        lax.all_gather(new_key.astype(jnp.bfloat16), "batch", axis=0, tiled=True),
        lax.all_gather(new_value.astype(jnp.bfloat16), "batch", axis=0, tiled=True),
        lax.all_gather(new_mixed.astype(jnp.bfloat16), "batch", axis=1, tiled=True),
        lax.all_gather(new_norm.astype(jnp.bfloat16), "batch", axis=0, tiled=True),
    )
    return (
        copy_up,
        copy_down,
        copy_query,
        copy_key,
        copy_value,
        copy_mixed,
        copy_norm,
        new_up,
        new_down,
        new_query,
        new_key,
        new_value,
        new_mixed,
        new_norm,
        state_new_up,
        state_new_down,
        state_new_query,
        state_new_key,
        state_new_value,
        state_new_mixed,
        state_new_norm,
    )


def solution(mesh):
    in_specs = (
        P("batch", None, "cols"),
        P("batch", "cols", None),
        P("batch", None, "cols"),
        P("batch", None, "cols"),
        P("batch", None, "cols"),
        P("batch", "cols", None),
        P("batch", None),
        P("batch", "cols"),
        P("cols", "batch"),
        P("batch", "cols"),
        P("batch", "cols"),
        P("batch", "cols"),
        P("cols", "batch"),
        P("batch"),
        P("batch", "cols"),
        P("cols", "batch"),
        P("batch", "cols"),
        P("batch", "cols"),
        P("batch", "cols"),
        P("cols", "batch"),
        P("batch"),
    )
    out_specs = (
        P(None, "cols"),
        P("cols", None),
        P(None, "cols"),
        P(None, "cols"),
        P(None, "cols"),
        P("cols", None),
        P(),
        P("batch", "cols"),
        P("cols", "batch"),
        P("batch", "cols"),
        P("batch", "cols"),
        P("batch", "cols"),
        P("cols", "batch"),
        P("batch"),
        P("batch", "cols"),
        P("cols", "batch"),
        P("batch", "cols"),
        P("batch", "cols"),
        P("batch", "cols"),
        P("cols", "batch"),
        P("batch"),
    )
    return jax.shard_map(body, mesh=mesh, in_specs=in_specs, out_specs=out_specs, check_vma=False)
```

profile of v0, /device:TPU:1, one launch (start us, length us, event | category | flops | bytes accessed | tf_op | source)
XLA Modules:
  0.0 326.7 jit_solution(14137713241253828921)
XLA Ops:
  7.2 3.8 %convert_bitcast_fusion.1 = bf16[1024,1024]{1,0:T(8,128)(2,1)} fusion(f32[1,1024,1024]{2,1,0:T(8,128)} %param.21), kind=kLoop, calls=%fused_computation.1 | loop fusion | flops 1048576 | bytes 6291456 | tf_op jit(solution)/shard_map/convert_element_type | solution.py:35
  11.1 2.5 convert_bitcast_fusion
  13.7 2.6 copy.42
  16.3 1.1 copy-done.1
  17.5 0.8 convert_bitcast_fusion.5
  18.4 0.8 convert_bitcast_fusion.4
  19.3 0.8 convert_bitcast_fusion.3
  20.3 1.0 copy.44
  21.4 33.5 %reduce-scatter.11.cloned.1.call-done = bf16[128,1024]{1,0:T(8,128)(2,1)} async-done(((bf16[1024,1024]{1,0:T(8,128)(2,1)}), bf16[128,1024]{1,0:T(8,128)(2,1)}) %reduce-scatter.11.cloned.1.call-update) | async-done | bytes 262160 | tf_op jit(solution)/shard_map/reduce_scatter | solution.py:34
  54.9 2.1 fusion.5
  57.1 42.7 %reduce-scatter.19.cloned.1.call-done = bf16[128,1024]{1,0:T(8,128)(2,1)} async-done(((bf16[1024,1024]{1,0:T(8,128)(2,1)}), bf16[128,1024]{1,0:T(8,128)(2,1)}) %reduce-scatter.19.cloned.1.call-update) | async-done | bytes 262160
  99.9 1.1 copy.43
  101.1 1.2 fusion.4
  102.3 12.1 %psum.7 = f32[1024]{0:T(1024)S(1)} all-reduce(f32[1024]{0:T(1024)S(1)} %bitcast.24), channel_id=1, replica_groups=mesh['batch'=8,'cols'=4] {'batch'}, use_global_device_ids=true, to_apply=%region_6.0 | all-reduce | flops 1024 | bytes 8192 | tf_op jit(solution)/shard_map/psum | solution.py:53
  115.0 9.9 %all-gather = bf16[8,1,128]{2,1,0:T(2,128)(2,1)S(1)} all-gather(bf16[1,1,128]{2,1,0:T(2,128)(2,1)S(1)} %get-tuple-element.21), channel_id=1, replica_groups=mesh['batch'=8,'cols'=4] {'batch'}, dimensions={0}, use_global_device_ids=true | all-gather | bytes 2304 | tf_op jit(solution)/shard_map/all_gather | solution.py:87
  125.6 11.7 %reduce-scatter.13.cloned.1.call-done = bf16[128,256]{1,0:T(8,128)(2,1)} async-done(((bf16[1024,256]{1,0:T(8,128)(2,1)}), bf16[128,256]{1,0:T(8,128)(2,1)}) %reduce-scatter.13.cloned.1.call-update) | async-done | bytes 65552 | tf_op jit(solution)/shard_map/reduce_scatter | solution.py:40
  137.3 1.6 fusion.3
  138.9 10.9 %all_gather.23 = bf16[1024,256]{1,0:T(8,128)(2,1)S(1)} all-gather(bf16[128,256]{1,0:T(8,128)(2,1)S(1)} %get-tuple-element.33), channel_id=1, replica_groups=mesh['batch'=8,'cols'=4] {'batch'}, dimensions={0}, use_global_device_ids=true | all-gather | bytes 589824 | tf_op jit(solution)/shard_map/all_gather | solution.py:83
  149.7 25.2 %reduce-scatter.15.cloned.1.call-done = bf16[128,256]{1,0:T(8,128)(2,1)} async-done(((bf16[1024,256]{1,0:T(8,128)(2,1)}), bf16[128,256]{1,0:T(8,128)(2,1)}) %reduce-scatter.15.cloned.1.call-update) | async-done | bytes 65552 | tf_op jit(solution)/shard_map/reduce_scatter | solution.py:43
  175.0 1.6 fusion.2
  176.5 10.9 %all_gather.24 = bf16[1024,256]{1,0:T(8,128)(2,1)S(1)} all-gather(bf16[128,256]{1,0:T(8,128)(2,1)S(1)} %get-tuple-element.30), channel_id=1, replica_groups=mesh['batch'=8,'cols'=4] {'batch'}, dimensions={0}, use_global_device_ids=true | all-gather | bytes 589824 | tf_op jit(solution)/shard_map/all_gather | solution.py:84
  187.4 25.2 %reduce-scatter.17.cloned.1.call-done = bf16[128,256]{1,0:T(8,128)(2,1)} async-done(((bf16[1024,256]{1,0:T(8,128)(2,1)}), bf16[128,256]{1,0:T(8,128)(2,1)}) %reduce-scatter.17.cloned.1.call-update) | async-done | bytes 65552 | tf_op jit(solution)/shard_map/reduce_scatter | solution.py:46
  212.6 1.6 fusion.1
  214.2 10.9 %all_gather.25 = bf16[1024,256]{1,0:T(8,128)(2,1)S(1)} all-gather(bf16[128,256]{1,0:T(8,128)(2,1)S(1)} %get-tuple-element.27), channel_id=1, replica_groups=mesh['batch'=8,'cols'=4] {'batch'}, dimensions={0}, use_global_device_ids=true | all-gather | bytes 589824 | tf_op jit(solution)/shard_map/all_gather | solution.py:85
  225.1 25.2 %reduce-scatter.21.cloned.1.call-done = bf16[128,256]{1,0:T(8,128)(2,1)} async-done(((bf16[1024,256]{1,0:T(8,128)(2,1)}), bf16[128,256]{1,0:T(8,128)(2,1)}) %reduce-scatter.21.cloned.1.call-update) | async-done | bytes 65552
  250.3 0.9 copy.45
  252.0 11.0 %all_gather.26 = bf16[256,1024]{1,0:T(8,128)(2,1)S(1)} all-gather(bf16[256,128]{1,0:T(8,128)(2,1)S(1)} %get-tuple-element.24), channel_id=1, replica_groups=mesh['batch'=8,'cols'=4] {'batch'}, dimensions={1}, use_global_device_ids=true | all-gather | bytes 589824 | tf_op jit(solution)/shard_map/all_gather | solution.py:86
  263.0 18.5 %all-gather.4.cloned.1.call-done = bf16[1024,1024]{1,0:T(8,128)(2,1)} async-done(((bf16[128,1024]{1,0:T(8,128)(2,1)}), bf16[1024,1024]{1,0:T(8,128)(2,1)}) %all-gather.4.cloned.1.call-update) | async-done | bytes 2097168 | tf_op jit(solution)/shard_map/all_gather | solution.py:81
  281.5 30.6 %all-gather.6.cloned.1.call-done = bf16[1024,1024]{1,0:T(8,128)(2,1)} async-done(((bf16[1024,128]{1,0:T(8,128)(2,1)}), bf16[1024,1024]{1,0:T(8,128)(2,1)}) %all-gather.6.cloned.1.call-update) | async-done | bytes 2097168 | tf_op jit(solution)/shard_map/all_gather | solution.py:82
  312.1 3.2 copy.52
  315.4 1.3 copy.53
  317.5 0.8 copy.55
  (62 shorter events, 4.9 us)
Async XLA Ops:
  7.2 47.7 %reduce-scatter.11.cloned.1.call-start = ((), (), s32[]{:S(2)}) async-start(), calls=%async_computation.6 | async-start | bytes 2359296 | tf_op jit(solution)/shard_map/reduce_scatter | solution.py:34
  11.1 88.8 %reduce-scatter.19.cloned.1.call-start = ((), (), s32[]{:S(2)}) async-start(), calls=%async_computation.12 | async-start | bytes 2359296
  16.2 1.2 copy-start.1
  16.2 2.2 copy-start.2
  16.3 3.1 copy-start.3
  16.3 121.0 %reduce-scatter.13.cloned.1.call-start = ((), (), s32[]{:S(2)}) async-start(), calls=%async_computation.9 | async-start | bytes 589824 | tf_op jit(solution)/shard_map/reduce_scatter | solution.py:40
  18.3 1.9 copy-start.4
  18.3 156.6 %reduce-scatter.15.cloned.1.call-start = ((), (), s32[]{:S(2)}) async-start(), calls=%async_computation.10 | async-start | bytes 589824 | tf_op jit(solution)/shard_map/reduce_scatter | solution.py:43
  19.3 193.4 %reduce-scatter.17.cloned.1.call-start = ((), (), s32[]{:S(2)}) async-start(), calls=%async_computation.11 | async-start | bytes 589824 | tf_op jit(solution)/shard_map/reduce_scatter | solution.py:46
  20.2 34.7 %copy-start.5 = (f32[128,1024]{1,0:T(8,128)S(1)}, f32[128,1024]{1,0:T(8,128)}, u32[]{:S(2)}) copy-start(f32[128,1024]{1,0:T(8,128)} %param.28) | copy-start | bytes 1572868
  20.2 34.7 %copy-start.6 = (f32[128,1024]{1,0:T(8,128)S(1)}, f32[128,1024]{1,0:T(8,128)}, u32[]{:S(2)}) copy-start(f32[128,1024]{1,0:T(8,128)} %param.35) | copy-start | bytes 1572868
  20.2 230.1 %reduce-scatter.21.cloned.1.call-start = ((), (), s32[]{:S(2)}) async-start(), calls=%async_computation.13 | async-start | bytes 589824
  21.3 79.7 %copy-start.7 = (f32[1024,128]{1,0:T(8,128)S(1)}, f32[1024,128]{1,0:T(8,128)}, u32[]{:S(2)}) copy-start(f32[1024,128]{1,0:T(8,128)} %param.29) | copy-start | bytes 1572868
  21.3 79.7 %copy-start.8 = (f32[1024,128]{1,0:T(8,128)S(1)}, f32[1024,128]{1,0:T(8,128)}, u32[]{:S(2)}) copy-start(f32[1024,128]{1,0:T(8,128)} %param.36) | copy-start | bytes 1572868
  21.4 260.2 %all-gather.4.cloned.1.call-start = ((), (), s32[]{:S(2)}) async-start(), calls=%async_computation.7 | async-start | bytes 2359296 | tf_op jit(solution)/shard_map/all_gather | solution.py:81
  57.0 45.2 %copy-start.17 = (f32[1,1024]{1,0:T(1,128)S(1)}, f32[1,1024]{1,0:T(1,128)}, u32[]{:S(2)}) copy-start(f32[1,1024]{1,0:T(1,128)} %param.27) | copy-start | bytes 12292
  57.0 57.4 %copy-start.18 = (f32[128]{0:T(128)S(1)}, f32[128]{0:T(128)}, u32[]{:S(2)}) copy-start(f32[128]{0:T(128)} %param.34) | copy-start | bytes 1540
  57.0 57.4 %copy-start.19 = (f32[128]{0:T(128)S(1)}, f32[128]{0:T(128)}, u32[]{:S(2)}) copy-start(f32[128]{0:T(128)} %param.41) | copy-start | bytes 1540
  57.0 80.3 %copy-start.9 = (f32[128,256]{1,0:T(8,128)S(1)}, f32[128,256]{1,0:T(8,128)}, u32[]{:S(2)}) copy-start(f32[128,256]{1,0:T(8,128)} %param.30) | copy-start | bytes 393220
  57.1 80.3 %copy-start.10 = (f32[128,256]{1,0:T(8,128)S(1)}, f32[128,256]{1,0:T(8,128)}, u32[]{:S(2)}) copy-start(f32[128,256]{1,0:T(8,128)} %param.37) | copy-start | bytes 393220
  57.1 255.0 %all-gather.6.cloned.1.call-start = ((), (), s32[]{:S(2)}) async-start(), calls=%async_computation.8 | async-start | bytes 2359296 | tf_op jit(solution)/shard_map/all_gather | solution.py:82
  101.0 74.0 %copy-start.11 = (f32[128,256]{1,0:T(8,128)S(1)}, f32[128,256]{1,0:T(8,128)}, u32[]{:S(2)}) copy-start(f32[128,256]{1,0:T(8,128)} %param.31) | copy-start | bytes 393220
  101.0 73.9 %copy-start.12 = (f32[128,256]{1,0:T(8,128)S(1)}, f32[128,256]{1,0:T(8,128)}, u32[]{:S(2)}) copy-start(f32[128,256]{1,0:T(8,128)} %param.38) | copy-start | bytes 393220
  101.0 111.6 %copy-start.13 = (f32[128,256]{1,0:T(8,128)S(1)}, f32[128,256]{1,0:T(8,128)}, u32[]{:S(2)}) copy-start(f32[128,256]{1,0:T(8,128)} %param.32) | copy-start | bytes 393220
  101.0 111.6 %copy-start.14 = (f32[128,256]{1,0:T(8,128)S(1)}, f32[128,256]{1,0:T(8,128)}, u32[]{:S(2)}) copy-start(f32[128,256]{1,0:T(8,128)} %param.39) | copy-start | bytes 393220
  102.2 149.0 %copy-start.15 = (f32[256,128]{1,0:T(8,128)S(1)}, f32[256,128]{1,0:T(8,128)}, u32[]{:S(2)}) copy-start(f32[256,128]{1,0:T(8,128)} %param.33) | copy-start | bytes 393220
  102.2 149.0 %copy-start.16 = (f32[256,128]{1,0:T(8,128)S(1)}, f32[256,128]{1,0:T(8,128)}, u32[]{:S(2)}) copy-start(f32[256,128]{1,0:T(8,128)} %param.40) | copy-start | bytes 393220
  312.1 3.2 copy-start
Sparse Core Ops, SparseCore 0:
  11.9 42.9 reduce-scatter.10
  58.7 41.0 reduce-scatter.18
  103.5 33.7 reduce-scatter.12
  140.8 34.1 reduce-scatter.14
  178.5 34.1 reduce-scatter.16
  216.1 34.1 reduce-scatter.20
  252.8 28.7 all-gather.3
  284.0 28.1 all-gather.5
where the time goes:
time: 327 us
  waiting for transfers between devices  213 us (65%)
  blocking collectives  65.6 us (20%)
  other arithmetic  18.9 us (6%)
  local copies, waits for them, and re-layouts  14.6 us (4%)
  between operations  14.4 us (4%)
    unnamed x10, waiting for transfers between devices  68.1 us
    reduce_scatter x1, waiting for transfers between devices, body(): lax.psum_scatter(grad_up[0].astype(jnp.bfloat16), 'batch', scatter_dimens...  33.5 us
    all_gather x1, waiting for transfers between devices, body(): lax.all_gather(new_down.astype(jnp.bfloat16), 'batch', axis=1, tiled=True)  30.6 us
    reduce_scatter x1, waiting for transfers between devices, body(): lax.psum_scatter(grad_key[0].astype(jnp.bfloat16), 'batch', scatter_dimen...  25.2 us
    reduce_scatter x1, waiting for transfers between devices, body(): lax.psum_scatter(grad_value[0].astype(jnp.bfloat16), 'batch', scatter_dim...  25.2 us
    all_gather x1, waiting for transfers between devices, body(): lax.all_gather(new_up.astype(jnp.bfloat16), 'batch', axis=0, tiled=True)  18.5 us
    unnamed x50, local copies, waits for them, and re-layouts  14.6 us
    psum x1, blocking collectives, body(): whole_norm = lax.psum(grad_norm[0], 'batch')  12.1 us
  transfers between devices with their start and end apart: 8, of which 8 were waited for; matrix products, arithmetic and copies ran while one was open for 6% of the time, Pallas kernels for 0%

commit v1 on v0

--- a/solution.py
+++ b/solution.py
@@ -1,6 +1,10 @@
+import functools
+
 import jax
 import jax.numpy as jnp
 from jax import lax
+from jax.experimental import pallas as pl
+from jax.experimental.pallas import tpu as pltpu
 from jax.sharding import PartitionSpec as P
 
 learn_rate = 0.1
@@ -111,6 +115,387 @@
     )
 
 
+PIECES = (4, 4, 1, 1, 1, 1)
+X_FIRST = (0, 2, 3)
+Y_FIRST = (1, 5, 4)
+BY_ROWS = (True, False, True, True, True, False)
+LOAD, SEND, RECV, OWN, NEW, STATE, KINDS = 0, 1, 7, 13, 14, 15, 16
+
+
+def pieces_of(shapes):
+    lists = []
+    for names, x_first in ((X_FIRST, True), (Y_FIRST, False)):
+        lists.append([])
+        for m in names:
+            rows = shapes[m][0] // PIECES[m]
+            for k in range(PIECES[m]):
+                lists[-1].append((m, k, rows, x_first))
+    return lists
+
+
+def exchange(shapes, n, *refs):
+    refs = list(refs)
+
+    def take(count):
+        out, refs[:] = refs[:count], refs[count:]
+        return out
+
+    grads, weights, moments = take(6), take(6), take(6)
+    grad_norm, weight_norm, moment_norm = take(3)
+    gathered, news, states = take(6), take(6), take(6)
+    norm_pack, norm_out = take(2)
+    grad_v, weight_v, moment_v, new_v, state_v = (take(6) for _ in range(5))
+    send_1, recv_1, send_2, recv_2, keep_2 = (take(6) for _ in range(5))
+    send_3, recv_3, keep_3, own_v = (take(6) for _ in range(4))
+    norm_send, norm_recv, norm_all = take(3)
+    sems, param_sems, norm_sems, norm_sems_2 = take(4)
+
+    me = lax.axis_index("batch")
+    c = lax.rem(me, 2)
+    x = lax.rem(lax.div(me, 2), 2)
+    y = lax.div(me, 4)
+    other_c, other_x, other_y = me + 1 - 2 * c, me + 2 - 4 * x, me + 4 - 8 * y
+    rate = n ** (-0.5)
+
+    lists = pieces_of(shapes)
+    pairs = len(lists[0])
+    number = {}
+    for p in range(pairs):
+        for s in range(2):
+            number[lists[s][p][:2]] = 2 * p + s
+
+    def sem(piece, kind):
+        return sems.at[number[piece[:2]], kind]
+
+    def load(piece):
+        m, k, rows, _ = piece
+        at = pl.ds(k * rows, rows)
+        if BY_ROWS[m]:
+            source, target = grads[m].at[:, at, :], grad_v[m].at[:, at, :]
+        else:
+            source, target = grads[m].at[at, :], grad_v[m].at[at, :]
+        return pltpu.make_async_copy(source, target, sem(piece, LOAD))
+
+    def params(m):
+        return (
+            pltpu.make_async_copy(weights[m], weight_v[m], param_sems.at[m, 0]),
+            pltpu.make_async_copy(moments[m], moment_v[m], param_sems.at[m, 1]),
+        )
+
+    def remote(piece, step, source, target, device):
+        return pltpu.make_async_remote_copy(
+            src_ref=source,
+            dst_ref=target,
+            send_sem=sem(piece, SEND + step),
+            recv_sem=sem(piece, RECV + step),
+            device_id={"batch": device},
+            device_id_type=pl.DeviceIdType.MESH,
+        )
+
+    def hop(piece, step):
+        m, k, rows, x_first = piece
+        first, second = (other_x, other_y) if x_first else (other_y, other_x)
+        place = gathered[m]
+        if step == 0:
+            return remote(piece, 0, send_1[m].at[k], recv_1[m].at[k], other_c)
+        if step == 1:
+            return remote(piece, 1, send_2[m].at[k], recv_2[m].at[k], first)
+        if step == 2:
+            return remote(piece, 2, send_3[m].at[k], recv_3[m].at[k], second)
+        if step == 3:
+            return remote(piece, 3, own_v[m].at[k], place.at[k, y, x, c], second)
+        if step == 4:
+            part = place.at[k, :, x, c] if x_first else place.at[k, y, :, c]
+            return remote(piece, 4, part, part, first)
+        part = place.at[k, :, :, c]
+        return remote(piece, 5, part, part, other_c)
+
+    def own_copies(piece):
+        m, k, rows, _ = piece
+        at = pl.ds(k * rows, rows)
+        return (
+            pltpu.make_async_copy(own_v[m].at[k], gathered[m].at[k, y, x, c], sem(piece, OWN)),
+            pltpu.make_async_copy(new_v[m].at[at, :], news[m].at[at, :], sem(piece, NEW)),
+            pltpu.make_async_copy(state_v[m].at[at, :], states[m].at[at, :], sem(piece, STATE)),
+        )
+
+    def block(piece, owner):
+        m, k, rows, _ = piece
+        at = pl.ds(k * rows, rows)
+        if BY_ROWS[m]:
+            return grad_v[m][owner, at, :]
+        width = shapes[m][1]
+        return grad_v[m][at, pl.ds(pl.multiple_of(owner * width, width), width)]
+
+    def stage(piece, step):
+        m, k, rows, x_first = piece
+        f, s = (x, y) if x_first else (y, x)
+
+        def spot(first, second):
+            return 2 * second + first if x_first else 2 * first + second
+
+        if step == 0:
+            load(piece).wait()
+            for q in range(4):
+                send_1[m][k, q] = block(piece, 2 * q + 1 - c).astype(jnp.bfloat16)
+            hop(piece, 0).start()
+        elif step == 1:
+            hop(piece, 0).wait_recv()
+            for second in range(2):
+                q = spot(1 - f, second)
+                total = block(piece, 2 * q + c) + recv_1[m][k, q].astype(jnp.float32)
+                send_2[m][k, second] = total.astype(jnp.bfloat16)
+            hop(piece, 1).start()
+            for second in range(2):
+                q = spot(f, second)
+                keep_2[m][k, second] = block(piece, 2 * q + c) + recv_1[m][k, q].astype(jnp.float32)
+        elif step == 2:
+            hop(piece, 1).wait_recv()
+            total = keep_2[m][k, 1 - s] + recv_2[m][k, 1 - s].astype(jnp.float32)
+            send_3[m][k] = total.astype(jnp.bfloat16)
+            hop(piece, 2).start()
+            keep_3[m][k] = keep_2[m][k, s] + recv_2[m][k, s].astype(jnp.float32)
+        elif step == 3:
+            if k == 0:
+                for copy in params(m):
+                    copy.wait()
+            hop(piece, 2).wait_recv()
+            at = pl.ds(k * rows, rows)
+            mean = (keep_3[m][k] + recv_3[m][k].astype(jnp.float32)) * rate
+            state = hold_rate * moment_v[m][at, :] + mean
+            new = weight_v[m][at, :] - learn_rate * state
+            own_v[m][k] = new.astype(jnp.bfloat16)
+            hop(piece, 3).start()
+            new_v[m][at, :] = new
+            state_v[m][at, :] = state
+            for copy in own_copies(piece):
+                copy.start()
+        elif step == 4:
+            own_copies(piece)[0].wait()
+            hop(piece, 3).wait_recv()
+            hop(piece, 4).start()
+        elif step == 5:
+            hop(piece, 4).wait_recv()
+            hop(piece, 5).start()
+        else:
+            hop(piece, 5).wait_recv()
+
+    started = set()
+    for p in range(pairs):
+        for s in range(2):
+            load(lists[s][p]).start()
+        if p >= 1:
+            for s in range(2):
+                m = lists[s][p - 1][0]
+                if m not in started:
+                    started.add(m)
+                    for copy in params(m):
+                        copy.start()
+    for m in range(6):
+        if m not in started:
+            for copy in params(m):
+                copy.start()
+
+    barrier = pltpu.get_barrier_semaphore()
+    for d in range(1, n):
+        pl.semaphore_signal(
+            barrier, inc=1, device_id={"batch": lax.rem(me + d, n)}, device_id_type=pl.DeviceIdType.MESH
+        )
+    pl.semaphore_wait(barrier, n - 1)
+
+    width = weight_norm.shape[1]
+
+    def norm_hop(d):
+        to = lax.rem(me + d, n)
+        return pltpu.make_async_remote_copy(
+            src_ref=norm_send.at[to],
+            dst_ref=norm_recv.at[d],
+            send_sem=norm_sems.at[0, d],
+            recv_sem=norm_sems.at[1, d],
+            device_id={"batch": to},
+            device_id_type=pl.DeviceIdType.MESH,
+        )
+
+    def norm_back(d):
+        to = lax.rem(me + d, n)
+        return pltpu.make_async_remote_copy(
+            src_ref=norm_pack.at[0],
+            dst_ref=norm_all.at[d],
+            send_sem=norm_sems_2.at[0, d],
+            recv_sem=norm_sems_2.at[1, d],
+            device_id={"batch": to},
+            device_id_type=pl.DeviceIdType.MESH,
+        )
+
+    def norm_start():
+        for j in range(n):
+            part = grad_norm[:, j * width : (j + 1) * width]
+            norm_send[j] = jnp.broadcast_to(part, (8, width))
+        for d in range(1, n):
+            norm_hop(d).start()
+
+    def norm_update():
+        total = norm_send[me]
+        for d in range(1, n):
+            norm_hop(d).wait_recv()
+            total = total + norm_recv[d]
+        state = hold_rate * moment_norm[...] + total * rate
+        norm_pack[1] = state
+        norm_pack[0] = weight_norm[...] - learn_rate * state
+        for d in range(1, n):
+            norm_back(d).start()
+
+    def norm_end():
+        norm_out[me] = norm_pack[0]
+        for d in range(1, n):
+            norm_back(d).wait_recv()
+            norm_out[lax.rem(me + n - d, n)] = norm_all[d]
+
+    for slot in range(pairs + 6):
+        for step in range(6, -1, -1):
+            p = slot - step
+            if 0 <= p < pairs:
+                for s in range(2):
+                    stage(lists[s][p], step)
+        if slot == 1:
+            norm_start()
+        if slot == 3:
+            norm_update()
+    norm_end()
+
+    for p in range(pairs):
+        for s in range(2):
+            piece = lists[s][p]
+            for step in range(6):
+                hop(piece, step).wait_send()
+            for copy in own_copies(piece)[1:]:
+                copy.wait()
+    for d in range(1, n):
+        norm_hop(d).wait_send()
+        norm_back(d).wait_send()
+
+
+def write_out(shapes, n, *refs):
+    refs = list(refs)
+
+    def take(count):
+        out, refs[:] = refs[:count], refs[count:]
+        return out
+
+    gathered, news, states = take(6), take(6), take(6)
+    norm_pack, norm_out = take(2)
+    copies, new_outs, state_outs = take(6), take(6), take(6)
+    copy_norm, new_norm, state_norm = take(3)
+    (sems,) = take(1)
+    started = []
+    count = 0
+    for m in range(6):
+        rows = shapes[m][0] // PIECES[m]
+        width = shapes[m][1]
+        for k in range(PIECES[m]):
+            for j in range(n):
+                source = gathered[m].at[k, j // 4, j // 2 % 2, j % 2]
+                if BY_ROWS[m]:
+                    target = copies[m].at[pl.ds(j * shapes[m][0] + k * rows, rows), :]
+                else:
+                    target = copies[m].at[pl.ds(k * rows, rows), pl.ds(j * width, width)]
+                started.append(pltpu.make_async_copy(source, target, sems.at[count]))
+                count += 1
+        for source, target in ((news[m], new_outs[m]), (states[m], state_outs[m])):
+            started.append(pltpu.make_async_copy(source, target, sems.at[count]))
+            count += 1
+    for copy in started:
+        copy.start()
+    for j in range(n):
+        width = norm_out.shape[2]
+        copy_norm[:, j * width : (j + 1) * width] = norm_out[j, 0:1, :].astype(jnp.bfloat16)
+    new_norm[...] = norm_pack[0, 0:1, :]
+    state_norm[...] = norm_pack[1, 0:1, :]
+    for copy in started:
+        copy.wait()
+
+
+def kernel_body(*args):
+    n = lax.axis_size("batch")
+    grads, grad_norm = [a[0] for a in args[:6]], args[6]
+    weights, weight_norm = args[7:13], args[13]
+    moments, moment_norm = args[14:20], args[20]
+    shapes = [w.shape for w in weights]
+    grads = [g.reshape((n, *s)) if by_rows else g for g, s, by_rows in zip(grads, shapes, BY_ROWS)]
+    width = weight_norm.shape[0]
+    bf16, f32 = jnp.bfloat16, jnp.float32
+    any_spec = pl.BlockSpec(memory_space=pl.ANY)
+    vmem_spec = pl.BlockSpec(memory_space=pltpu.VMEM)
+    hbm_spec = pl.BlockSpec(memory_space=pltpu.HBM)
+
+    def cut(m):
+        rows, cols = shapes[m]
+        return PIECES[m], rows // PIECES[m], cols
+
+    every = range(6)
+
+    def scratch(lead, kind):
+        return [pltpu.VMEM((cut(m)[0], *lead, *cut(m)[1:]), kind) for m in every]
+
+    whole = [pltpu.VMEM(s, f32) for s in shapes]
+    held = [pltpu.VMEM((cut(m)[0], 2, 2, 2, *cut(m)[1:]), bf16) for m in every] + whole + whole
+    lists = pieces_of(shapes)
+    assert len(lists[0]) == len(lists[1])
+    results = pl.pallas_call(
+        functools.partial(exchange, shapes, n),
+        out_shape=held
+        + [jax.ShapeDtypeStruct((2, 8, width), f32), jax.ShapeDtypeStruct((n, 8, width), f32)],
+        in_specs=[any_spec] * 18 + [vmem_spec] * 3,
+        out_specs=[any_spec] * 18 + [vmem_spec] * 2,
+        scratch_shapes=[pltpu.VMEM(g.shape, f32) for g in grads]
+        + whole * 4
+        + scratch((4,), bf16) * 2
+        + scratch((2,), bf16) * 2
+        + scratch((2,), f32)
+        + scratch((), bf16) * 2
+        + scratch((), f32)
+        + scratch((), bf16)
+        + [pltpu.VMEM((n, 8, width), f32)] * 3
+        + [
+            pltpu.SemaphoreType.DMA((2 * len(lists[0]), KINDS)),
+            pltpu.SemaphoreType.DMA((6, 2)),
+            pltpu.SemaphoreType.DMA((2, n)),
+            pltpu.SemaphoreType.DMA((2, n)),
+        ],
+        compiler_params=pltpu.CompilerParams(
+            collective_id=0, has_side_effects=True, vmem_limit_bytes=40 * 2**20
+        ),
+    )(*grads, *weights, *moments, grad_norm, weight_norm.reshape(1, width), moment_norm.reshape(1, width))
+    copies = n * sum(PIECES) + 12
+    finals = pl.pallas_call(
+        functools.partial(write_out, shapes, n),
+        out_shape=[
+            jax.ShapeDtypeStruct((n * s[0], s[1]) if by_rows else (s[0], n * s[1]), bf16)
+            for s, by_rows in zip(shapes, BY_ROWS)
+        ]
+        + [jax.ShapeDtypeStruct(s, f32) for s in shapes] * 2
+        + [
+            jax.ShapeDtypeStruct((1, n * width), bf16),
+            jax.ShapeDtypeStruct((1, width), f32),
+            jax.ShapeDtypeStruct((1, width), f32),
+        ],
+        in_specs=[any_spec] * 18 + [vmem_spec] * 2,
+        out_specs=[hbm_spec] * 18 + [vmem_spec] * 3,
+        scratch_shapes=[pltpu.SemaphoreType.DMA((copies,))],
+        compiler_params=pltpu.CompilerParams(vmem_limit_bytes=8 * 2**20),
+    )(*[pltpu.with_memory_space_constraint(r, pltpu.VMEM) for r in results[:18]], *results[18:])
+    copy, new, state = finals[:6], finals[6:12], finals[12:18]
+    copy_norm, new_norm, state_norm = (r.reshape(r.shape[1]) for r in finals[18:])
+    return (*copy, copy_norm, *new, new_norm, *state, state_norm)
+
+
+def chosen(*args):
+    fits = lax.axis_size("batch") == 2**3 and args[13].shape[0] % 128 == 0
+    for w, count in zip(args[7:13], PIECES):
+        fits = fits and w.shape[0] % (16 * count) == 0 and w.shape[1] % 128 == 0
+    return kernel_body(*args) if fits else body(*args)
+
+
 def solution(mesh):
     in_specs = (
         P("batch", None, "cols"),
@@ -158,4 +543,4 @@
         P("cols", "batch"),
         P("batch"),
     )
-    return jax.shard_map(body, mesh=mesh, in_specs=in_specs, out_specs=out_specs, check_vma=False)
+    return jax.shard_map(chosen, mesh=mesh, in_specs=in_specs, out_specs=out_specs, check_vma=False)

time: 327 us -> 89.4 us (0.27)
  waiting for transfers between devices: 213 us -> 0 us
  Pallas kernels: 0 us -> 73 us
  blocking collectives: 65.6 us -> 0 us
  other arithmetic: 18.9 us -> 0.6 us
  between operations: 14.4 us -> 0.71 us
    reduce_scatter x4 -> x0, waiting for transfers between devices: 95.7 us -> none  [the longest x1 33.5 us: body(): lax.psum_scatter(grad_up[0].astype(jnp.bfloat16), 'batch', scatter_dimens...]
    pallas_call x0 -> x2, Pallas kernels: none -> 73 us  [the longest x1 67.9 us: kernel_body(): pl.pallas_call(functools.partial(exchange, shapes, n), out_shape=held + [...]
    unnamed x10 -> x0, waiting for transfers between devices: 68.1 us -> none
    all_gather x5 -> x0, blocking collectives: 53.5 us -> none  [the longest x1 11 us: body(): lax.all_gather(new_mixed.astype(jnp.bfloat16), 'batch', axis=1, tiled=True)]
    all_gather x2 -> x0, waiting for transfers between devices: 49.1 us -> none  [the longest x1 30.6 us: body(): lax.all_gather(new_down.astype(jnp.bfloat16), 'batch', axis=1, tiled=True)]
    convert_element_type x12 -> x0, other arithmetic: 17.7 us -> none  [the longest x1 3.84 us: body(): grad_up[0].astype(jnp.bfloat16)]
    psum x1 -> x0, blocking collectives: 12.1 us -> none  [body(): whole_norm = lax.psum(grad_norm[0], 'batch')]
    unnamed x50 -> x32, local copies, waits for them, and re-layouts: 14.6 us -> 14.6 us
  transfers between devices with their start and end apart: 8 -> 0, of which waited for: 8 -> 0; matrix products, arithmetic and copies ran while one was open for 6% -> 0% of each run, Pallas kernels for 0% -> 0%
where the time goes in v1:
time: 89.4 us; the launch traced here: 88.9 us
  Pallas kernels  73 us (82%)
  local copies, waits for them, and re-layouts  14.6 us (16%)
    pallas_call x1, Pallas kernels, kernel_body(): pl.pallas_call(functools.partial(exchange, shapes, n), out_shape=held + [...  67.9 us
    unnamed x32, local copies, waits for them, and re-layouts  14.6 us
    pallas_call x1, Pallas kernels, kernel_body(): pl.pallas_call(functools.partial(write_out, shapes, n), out_shape=[jax.Sh...  5.07 us

profile of v1, /device:TPU:1, one launch (start us, length us, event | category | flops | bytes accessed | tf_op | source)
XLA Modules:
  0.0 88.9 jit_solution(9686891107359500631)
XLA Ops:
  0.7 0.0 copy-start
  0.7 1.2 %copy-done = f32[1,1024,256]{2,1,0:T(8,128)S(1)} copy-done((f32[1,1024,256]{2,1,0:T(8,128)S(1)}, f32[1,1024,256]{2,1,0:T(8,128)}, u32[]{:S(2)}) %copy-start) | copy-done | bytes 1048600
  1.9 0.0 copy-start.1
  1.9 1.0 %copy-done.1 = f32[128,1024]{1,0:T(8,128)S(1)} copy-done((f32[128,1024]{1,0:T(8,128)S(1)}, f32[128,1024]{1,0:T(8,128)}, u32[]{:S(2)}) %copy-start.1) | copy-done | bytes 524312
  2.9 1.0 %copy-done.2 = f32[1024,128]{1,0:T(8,128)S(1)} copy-done((f32[1024,128]{1,0:T(8,128)S(1)}, f32[1024,128]{1,0:T(8,128)}, u32[]{:S(2)}) %copy-start.2) | copy-done | bytes 524312
  4.0 0.0 copy-start.3
  4.0 1.0 %copy-done.3 = f32[128,1024]{1,0:T(8,128)S(1)} copy-done((f32[128,1024]{1,0:T(8,128)S(1)}, f32[128,1024]{1,0:T(8,128)}, u32[]{:S(2)}) %copy-start.3) | copy-done | bytes 524312
  5.0 0.0 copy-start.4
  5.0 1.0 %copy-done.4 = f32[1024,128]{1,0:T(8,128)S(1)} copy-done((f32[1024,128]{1,0:T(8,128)S(1)}, f32[1024,128]{1,0:T(8,128)}, u32[]{:S(2)}) %copy-start.4) | copy-done | bytes 524312
  6.1 0.0 copy-start.5
  6.1 0.9 %copy-done.5 = f32[128,256]{1,0:T(8,128)S(1)} copy-done((f32[128,256]{1,0:T(8,128)S(1)}, f32[128,256]{1,0:T(8,128)}, u32[]{:S(2)}) %copy-start.5) | copy-done | bytes 131096
  7.0 0.0 copy-start.6
  7.0 0.9 %copy-done.6 = f32[128,256]{1,0:T(8,128)S(1)} copy-done((f32[128,256]{1,0:T(8,128)S(1)}, f32[128,256]{1,0:T(8,128)}, u32[]{:S(2)}) %copy-start.6) | copy-done | bytes 131096
  7.9 0.0 copy-start.7
  7.9 0.9 %copy-done.7 = f32[128,256]{1,0:T(8,128)S(1)} copy-done((f32[128,256]{1,0:T(8,128)S(1)}, f32[128,256]{1,0:T(8,128)}, u32[]{:S(2)}) %copy-start.7) | copy-done | bytes 131096
  8.8 0.0 copy-start.8
  8.8 0.9 %copy-done.8 = f32[256,128]{1,0:T(8,128)S(1)} copy-done((f32[256,128]{1,0:T(8,128)S(1)}, f32[256,128]{1,0:T(8,128)}, u32[]{:S(2)}) %copy-start.8) | copy-done | bytes 131096
  9.7 0.0 copy-start.9
  9.7 0.9 %copy-done.9 = f32[128,256]{1,0:T(8,128)S(1)} copy-done((f32[128,256]{1,0:T(8,128)S(1)}, f32[128,256]{1,0:T(8,128)}, u32[]{:S(2)}) %copy-start.9) | copy-done | bytes 131096
  10.6 0.9 %copy-done.10 = f32[128,256]{1,0:T(8,128)S(1)} copy-done((f32[128,256]{1,0:T(8,128)S(1)}, f32[128,256]{1,0:T(8,128)}, u32[]{:S(2)}) %copy-start.10) | copy-done | bytes 131096
  11.5 0.0 copy-start.11
  11.5 0.9 %copy-done.11 = f32[128,256]{1,0:T(8,128)S(1)} copy-done((f32[128,256]{1,0:T(8,128)S(1)}, f32[128,256]{1,0:T(8,128)}, u32[]{:S(2)}) %copy-start.11) | copy-done | bytes 131096
  12.4 0.0 copy-start.12
  12.4 0.9 %copy-done.12 = f32[256,128]{1,0:T(8,128)S(1)} copy-done((f32[256,128]{1,0:T(8,128)S(1)}, f32[256,128]{1,0:T(8,128)}, u32[]{:S(2)}) %copy-start.12) | copy-done | bytes 131096
  13.3 0.0 copy-start.13
  13.3 0.7 copy-done.13
  14.0 0.0 copy-start.14
  14.0 0.7 copy-done.14
  14.6 0.7 copy-done.15
  15.3 67.9 %shard_map.364 = (bf16[4,2,2,2,32,1024]{5,4,3,2,1,0:T(8,128)(2,1)S(1)}, bf16[4,2,2,2,256,128]{5,4,3,2,1,0:T(8,128)(2,1)S(1)}, bf16[1,2,2,2,128,256]{5,4,3,2,1,0:...) custom-call(f32[8,128,1024]{2,1,0:T(8,128)} %bitcast.13, ...), custom_call_target="tpu_custom_call" | custom-call | tf_op jit(solution)/shard_map/pallas_call | solution.py:444
  83.2 5.1 %shard_map.365 = (bf16[1024,1024]{1,0:T(8,128)(2,1)}, bf16[1024,1024]{1,0:T(8,128)(2,1)}, bf16[1024,256]{1,0:T(8,128)(2,1)}, bf16[1024,256]{1,0:T(8,128)(2,1)}, ...) custom-call(bf16[4,2,2,2,32,1024]{5,4,3,2,1,0:T(8,128)(2,1)S(1)} %ge, ...), custom_call_target="tpu_custom_call" | custom-call | tf_op jit(solution)/shard_map/pallas_call | solution.py:470
  88.3 0.6 reduce
  (3 shorter events, 0.0 us)
Async XLA Ops:
  0.7 1.2 %copy-start = (f32[1,1024,256]{2,1,0:T(8,128)S(1)}, f32[1,1024,256]{2,1,0:T(8,128)}, u32[]{:S(2)}) copy-start(f32[1,1024,256]{2,1,0:T(8,128)} %param.23) | copy-start | bytes 3145732
  1.9 1.0 %copy-start.1 = (f32[128,1024]{1,0:T(8,128)S(1)}, f32[128,1024]{1,0:T(8,128)}, u32[]{:S(2)}) copy-start(f32[128,1024]{1,0:T(8,128)} %refs_6_.1) | copy-start | bytes 1572868
  2.9 1.0 %copy-start.2 = (f32[1024,128]{1,0:T(8,128)S(1)}, f32[1024,128]{1,0:T(8,128)}, u32[]{:S(2)}) copy-start(f32[1024,128]{1,0:T(8,128)} %refs_7_.1) | copy-start | bytes 1572868
  4.0 1.0 %copy-start.3 = (f32[128,1024]{1,0:T(8,128)S(1)}, f32[128,1024]{1,0:T(8,128)}, u32[]{:S(2)}) copy-start(f32[128,1024]{1,0:T(8,128)} %refs_12_.1) | copy-start | bytes 1572868
  5.0 1.0 %copy-start.4 = (f32[1024,128]{1,0:T(8,128)S(1)}, f32[1024,128]{1,0:T(8,128)}, u32[]{:S(2)}) copy-start(f32[1024,128]{1,0:T(8,128)} %refs_13_.1) | copy-start | bytes 1572868
  6.1 0.9 %copy-start.5 = (f32[128,256]{1,0:T(8,128)S(1)}, f32[128,256]{1,0:T(8,128)}, u32[]{:S(2)}) copy-start(f32[128,256]{1,0:T(8,128)} %refs_8_.1) | copy-start | bytes 393220
  7.0 0.9 %copy-start.6 = (f32[128,256]{1,0:T(8,128)S(1)}, f32[128,256]{1,0:T(8,128)}, u32[]{:S(2)}) copy-start(f32[128,256]{1,0:T(8,128)} %refs_9_.1) | copy-start | bytes 393220
  7.9 0.9 %copy-start.7 = (f32[128,256]{1,0:T(8,128)S(1)}, f32[128,256]{1,0:T(8,128)}, u32[]{:S(2)}) copy-start(f32[128,256]{1,0:T(8,128)} %refs_10_.1) | copy-start | bytes 393220
  8.8 0.9 %copy-start.8 = (f32[256,128]{1,0:T(8,128)S(1)}, f32[256,128]{1,0:T(8,128)}, u32[]{:S(2)}) copy-start(f32[256,128]{1,0:T(8,128)} %refs_11_.1) | copy-start | bytes 393220
  9.7 0.9 %copy-start.9 = (f32[128,256]{1,0:T(8,128)S(1)}, f32[128,256]{1,0:T(8,128)}, u32[]{:S(2)}) copy-start(f32[128,256]{1,0:T(8,128)} %refs_14_.1) | copy-start | bytes 393220
  10.6 0.9 %copy-start.10 = (f32[128,256]{1,0:T(8,128)S(1)}, f32[128,256]{1,0:T(8,128)}, u32[]{:S(2)}) copy-start(f32[128,256]{1,0:T(8,128)} %refs_15_.1) | copy-start | bytes 393220
  11.5 0.9 %copy-start.11 = (f32[128,256]{1,0:T(8,128)S(1)}, f32[128,256]{1,0:T(8,128)}, u32[]{:S(2)}) copy-start(f32[128,256]{1,0:T(8,128)} %refs_16_.1) | copy-start | bytes 393220
  12.4 0.9 %copy-start.12 = (f32[256,128]{1,0:T(8,128)S(1)}, f32[256,128]{1,0:T(8,128)}, u32[]{:S(2)}) copy-start(f32[256,128]{1,0:T(8,128)} %refs_17_.1) | copy-start | bytes 393220
  13.3 0.7 copy-start.13
  14.0 0.7 copy-start.14
  14.6 0.7 copy-start.15

commit v2 on v1

--- a/solution.py
+++ b/solution.py
@@ -116,6 +116,8 @@
 
 
 PIECES = (4, 4, 1, 1, 1, 1)
+DELAYS = (0, 1, 2, 3, 4, 5, 6)
+STEP_ORDER = (0, 1, 2, 3, 4, 5, 6)
 X_FIRST = (0, 2, 3)
 Y_FIRST = (1, 5, 4)
 BY_ROWS = (True, False, True, True, True, False)
@@ -141,14 +143,16 @@
         return out
 
     grads, weights, moments = take(6), take(6), take(6)
-    grad_norm, weight_norm, moment_norm = take(3)
+    norm_inputs = take(3)
     gathered, news, states = take(6), take(6), take(6)
     norm_pack, norm_out = take(2)
     grad_v, weight_v, moment_v, new_v, state_v = (take(6) for _ in range(5))
     send_1, recv_1, send_2, recv_2, keep_2 = (take(6) for _ in range(5))
     send_3, recv_3, keep_3, own_v = (take(6) for _ in range(4))
     norm_send, norm_recv, norm_all = take(3)
-    sems, param_sems, norm_sems, norm_sems_2 = take(4)
+    norm_held = take(3)
+    grad_norm, weight_norm, moment_norm = norm_held
+    sems, param_sems, norm_sems, norm_sems_2, norm_sems_3 = take(5)
 
     me = lax.axis_index("batch")
     c = lax.rem(me, 2)
@@ -327,7 +331,15 @@
             device_id_type=pl.DeviceIdType.MESH,
         )
 
+    def norm_loads():
+        return [
+            pltpu.make_async_copy(source, target, norm_sems_3.at[i])
+            for i, (source, target) in enumerate(zip(norm_inputs, norm_held))
+        ]
+
     def norm_start():
+        for copy in norm_loads():
+            copy.wait()
         for j in range(n):
             part = grad_norm[:, j * width : (j + 1) * width]
             norm_send[j] = jnp.broadcast_to(part, (8, width))
@@ -351,9 +363,11 @@
             norm_back(d).wait_recv()
             norm_out[lax.rem(me + n - d, n)] = norm_all[d]
 
-    for slot in range(pairs + 6):
-        for step in range(6, -1, -1):
-            p = slot - step
+    for copy in norm_loads():
+        copy.start()
+    for slot in range(pairs + DELAYS[-1]):
+        for step in STEP_ORDER:
+            p = slot - DELAYS[step]
             if 0 <= p < pairs:
                 for s in range(2):
                     stage(lists[s][p], step)
@@ -441,11 +455,13 @@
     held = [pltpu.VMEM((cut(m)[0], 2, 2, 2, *cut(m)[1:]), bf16) for m in every] + whole + whole
     lists = pieces_of(shapes)
     assert len(lists[0]) == len(lists[1])
+    norms = (grad_norm, weight_norm.reshape(1, width), moment_norm.reshape(1, width))
+    arrays = (*grads, *weights, *moments, *norms)
     results = pl.pallas_call(
         functools.partial(exchange, shapes, n),
         out_shape=held
         + [jax.ShapeDtypeStruct((2, 8, width), f32), jax.ShapeDtypeStruct((n, 8, width), f32)],
-        in_specs=[any_spec] * 18 + [vmem_spec] * 3,
+        in_specs=[any_spec] * 21,
         out_specs=[any_spec] * 18 + [vmem_spec] * 2,
         scratch_shapes=[pltpu.VMEM(g.shape, f32) for g in grads]
         + whole * 4
@@ -456,16 +472,19 @@
         + scratch((), f32)
         + scratch((), bf16)
         + [pltpu.VMEM((n, 8, width), f32)] * 3
+        + [pltpu.VMEM((1, n * width), f32)]
+        + [pltpu.VMEM((1, width), f32)] * 2
         + [
             pltpu.SemaphoreType.DMA((2 * len(lists[0]), KINDS)),
             pltpu.SemaphoreType.DMA((6, 2)),
             pltpu.SemaphoreType.DMA((2, n)),
             pltpu.SemaphoreType.DMA((2, n)),
+            pltpu.SemaphoreType.DMA((3,)),
         ],
         compiler_params=pltpu.CompilerParams(
             collective_id=0, has_side_effects=True, vmem_limit_bytes=40 * 2**20
         ),
-    )(*grads, *weights, *moments, grad_norm, weight_norm.reshape(1, width), moment_norm.reshape(1, width))
+    )(*[pltpu.with_memory_space_constraint(a, pltpu.HBM) for a in arrays])
     copies = n * sum(PIECES) + 12
     finals = pl.pallas_call(
         functools.partial(write_out, shapes, n),

time: 89.4 us -> 68.7 us (0.77)
  local copies, waits for them, and re-layouts: 14.6 us -> 0 us
  Pallas kernels: 73 us -> 67.2 us
    unnamed x32 -> x0, local copies, waits for them, and re-layouts: 14.6 us -> none
    pallas_call x1, Pallas kernels: 67.9 us -> 62.1 us  [kernel_body(): pl.pallas_call(functools.partial(exchange, shapes, n), out_shape=held + [...]
where the time goes in v2:
time: 68.7 us; the launch traced here: 68.5 us
  Pallas kernels  67.2 us (98%)
    pallas_call x1, Pallas kernels, kernel_body(): pl.pallas_call(functools.partial(exchange, shapes, n), out_shape=held + [...  62.1 us
    pallas_call x1, Pallas kernels, kernel_body(): pl.pallas_call(functools.partial(write_out, shapes, n), out_shape=[jax.Sh...  5.07 us

profile of v2, /device:TPU:1, one launch (start us, length us, event | category | flops | bytes accessed | tf_op | source)
XLA Modules:
  0.0 68.5 jit_solution(16261828131372978555)
XLA Ops:
  0.7 62.1 %shard_map.364 = (bf16[4,2,2,2,32,1024]{5,4,3,2,1,0:T(8,128)(2,1)S(1)}, bf16[4,2,2,2,256,128]{5,4,3,2,1,0:T(8,128)(2,1)S(1)}, bf16[1,2,2,2,128,256]{5,4,3,2,1,0:...) custom-call(f32[8,128,1024]{2,1,0:T(8,128)} %bitcast.10, ...), custom_call_target="tpu_custom_call" | custom-call | tf_op jit(solution)/shard_map/pallas_call | solution.py:460
  62.8 5.1 %shard_map.365 = (bf16[1024,1024]{1,0:T(8,128)(2,1)}, bf16[1024,1024]{1,0:T(8,128)(2,1)}, bf16[1024,256]{1,0:T(8,128)(2,1)}, bf16[1024,256]{1,0:T(8,128)(2,1)}, ...) custom-call(bf16[4,2,2,2,32,1024]{5,4,3,2,1,0:T(8,128)(2,1)S(1)} %ge, ...), custom_call_target="tpu_custom_call" | custom-call | tf_op jit(solution)/shard_map/pallas_call | solution.py:489
  67.9 0.6 reduce
